TPU v7x, 32 devices: a whole 2x2x4 slice. The times are simulated.
32 devices in a mesh: dp: 16 (over z, x, core), head: 2 (over y).
Axes of the slice: x: 2, y: 2, z: 4, core: 2. Of those that a mesh axis runs over, the one named last changes fastest.
Arguments:
- frames_in: bfloat16 [16, 2, 320, 2560], P('dp', 'head'), may hold values from -6 to 6
- ln1_gain: float32 [1280], replicated, may hold values from 0.25 to 1.75
- ln1_bias: float32 [1280], replicated, may hold values from -3 to 3
- qkv_weight: bfloat16 [1280, 3, 1024], P('dp', None, 'head'), may hold values from -0.1875 to 0.1875
- qv_bias: float32 [2, 1024], P(None, 'head'), may hold values from -3 to 3
- out_weight: bfloat16 [1024, 1280], P(('head', 'dp')), may hold values from -0.1875 to 0.1875
- out_bias: float32 [1280], P('head'), may hold values from -3 to 3
- ln2_gain: float32 [1280], replicated, may hold values from 0.25 to 1.75
- ln2_bias: float32 [1280], replicated, may hold values from -3 to 3
- fc1_weight: bfloat16 [1280, 5120], P('dp', 'head'), may hold values from -0.15625 to 0.15625
- fc1_bias: float32 [5120], P('head'), may hold values from -3 to 3
- fc2_weight: bfloat16 [5120, 1280], P(('head', 'dp')), may hold values from -0.078125 to 0.078125
- fc2_bias: float32 [1280], P('head'), may hold values from -3 to 3
- server_of_clip: int32 [16], replicated, may hold values from 0 to 7
Outputs:
- encoded: bfloat16 [16, 2, 320, 2560], P('dp', 'head')
All inputs are finite; a program needn't handle non-finite values.
Results may differ from a plain program's by a relative error of at most 0.014.
Values may be sent and summed in bfloat16 or wider, within the bound.
A program may use at most 64 MiB of HBM per device.

v0:
```python
import jax
import jax.numpy as jnp
from jax import lax
from jax.sharding import PartitionSpec as P

HDIM = 64
epsilon = 1e-05


def layer_norm(matrix, gain_row, shift_row):
    floats = matrix.astype(jnp.float32)
    center = jnp.mean(floats, axis=-1, keepdims=True)
    spread = jnp.mean(jnp.square(floats - center), axis=-1, keepdims=True)
    return ((floats - center) * lax.rsqrt(spread + epsilon) * gain_row + shift_row).astype(
        jnp.bfloat16
    )


def normalize(residual_in, gain_row, shift_row):
    whole_rows = lax.all_gather(residual_in, "head", axis=1, tiled=True)
    return layer_norm(whole_rows, gain_row, shift_row)


def attend(queries, key_rows, value_rows):

    def single(triple):
        query_head, key_head, value_head = triple
        scores = jnp.dot(query_head, key_head.T, preferred_element_type=jnp.float32)
        maxima = jnp.max(scores, axis=-1, keepdims=True)
        weights = jnp.exp(scores - maxima)
        probability = (weights / jnp.sum(weights, axis=-1, keepdims=True)).astype(jnp.bfloat16)
        return jnp.dot(probability, value_head, preferred_element_type=jnp.float32).astype(
            jnp.bfloat16
        )

    per_head = lax.map(
        single,
        (jnp.swapaxes(queries, 0, 1), jnp.swapaxes(key_rows, 0, 1), jnp.swapaxes(value_rows, 0, 1)),
    )
    return jnp.swapaxes(per_head, 0, 1).reshape(queries.shape[0], -1)


def slot_order(server_list):
    clip_count = server_list.shape[0]
    indices = jnp.arange(clip_count, dtype=jnp.int32)
    earlier = (server_list[None, :] < server_list[:, None]) | (
        server_list[None, :] == server_list[:, None]
    ) & (indices[None, :] < indices[:, None])
    slot_of = jnp.sum(earlier.astype(jnp.int32), axis=1)
    return jnp.sum(jnp.where(slot_of[None, :] == indices[:, None], indices[None, :], 0), axis=1)


def regroup(block_rows, clip_order):
    group_size = lax.axis_size("dp")
    piece_rows = block_rows.reshape(group_size, -1)
    shuffled = lax.all_to_all(piece_rows, "dp", split_axis=0, concat_axis=0, tiled=True)
    picked = jnp.take(shuffled, clip_order, axis=0)
    returned = lax.all_to_all(picked, "dp", split_axis=0, concat_axis=0, tiled=True)
    return returned.reshape(block_rows.shape)


def block_term(operand, weight_rows, row_count, frame_count, local_width):
    blocks = row_count // frame_count
    product = jnp.dot(operand, weight_rows, preferred_element_type=jnp.float32)
    return (
        product.reshape(frame_count, blocks, local_width)
        .transpose(1, 0, 2)
        .reshape(blocks * frame_count, local_width)
    )


def on_device(
    frames_in,
    ln1_gain,
    ln1_bias,
    qkv_weight,
    qv_bias,
    out_weight,
    out_bias,
    ln2_gain,
    ln2_bias,
    fc1_weight,
    fc1_bias,
    fc2_weight,
    fc2_bias,
    server_of_clip,
):
    clip_order = slot_order(server_of_clip)
    group_rows = frames_in.shape[2]
    local_width = frames_in.shape[3] // 4
    frame_count = group_rows * 4
    residual_in = frames_in[0, 0].reshape(frame_count, local_width)
    residual_in = regroup(residual_in, clip_order)
    normed_one = normalize(residual_in, ln1_gain, ln1_bias)
    column_count = qkv_weight.shape[2]
    weight_piece = lax.all_gather(qkv_weight, "dp", axis=0, tiled=True)
    operand = normed_one
    projected = jnp.dot(
        operand, weight_piece.reshape(weight_piece.shape[0], -1), preferred_element_type=jnp.float32
    ).reshape(frame_count, 3, column_count)
    queries = (
        ((projected[:, 0] + qv_bias[0]) * HDIM ** (-0.5))
        .astype(jnp.bfloat16)
        .reshape(frame_count, -1, HDIM)
    )
    key_rows = projected[:, 1].astype(jnp.bfloat16).reshape(frame_count, -1, HDIM)
    value_rows = (projected[:, 2] + qv_bias[1]).astype(jnp.bfloat16).reshape(frame_count, -1, HDIM)
    context = attend(queries, key_rows, value_rows)
    output_rows = lax.all_gather(out_weight, "dp", axis=0, tiled=True)
    carried = residual_in.astype(jnp.float32) + out_bias
    attended = (
        carried
        + lax.psum_scatter(
            block_term(
                context, output_rows, frame_count * lax.axis_size("head"), frame_count, local_width
            ).astype(jnp.bfloat16),
            "head",
            scatter_dimension=0,
            tiled=True,
        ).astype(jnp.float32)
    ).astype(jnp.bfloat16)
    normed_two = normalize(attended, ln2_gain, ln2_bias)
    operand = normed_two
    hidden_sums = jnp.dot(
        operand,
        lax.all_gather(fc1_weight, "dp", axis=0, tiled=True),
        preferred_element_type=jnp.float32,
    )
    hidden = jax.nn.gelu(hidden_sums + fc1_bias, approximate=False).astype(jnp.bfloat16)
    down_rows = lax.all_gather(fc2_weight, "dp", axis=0, tiled=True)
    kept = attended.astype(jnp.float32) + fc2_bias
    layer_out = (
        kept
        + lax.psum_scatter(
            block_term(
                hidden, down_rows, frame_count * lax.axis_size("head"), frame_count, local_width
            ).astype(jnp.bfloat16),
            "head",
            scatter_dimension=0,
            tiled=True,
        ).astype(jnp.float32)
    ).astype(jnp.bfloat16)
    return layer_out.reshape(1, 1, group_rows, 4 * local_width)


def solution(mesh):
    placed = (
        P("dp", "head", None, None),
        P(),
        P(),
        P("dp", None, "head"),
        P(None, "head"),
        P(("head", "dp"), None),
        P("head"),
        P(),
        P(),
        P("dp", "head"),
        P("head"),
        P(("head", "dp"), None),
        P("head"),
        P(),
    )
    return jax.shard_map(
        on_device,
        mesh=mesh,
        in_specs=placed,
        out_specs=P("dp", "head", None, None),
        check_vma=False,
    )
```

profile of v0, /device:TPU:0, one launch (start us, length us, event | category | flops | bytes accessed | tf_op | source)
XLA Modules:
  0.0 602.3 jit_solution(14963864365665853193)
XLA Ops:
  7.3 4.3 all_to_all.16
  12.1 11.7 %reduce.9 = bf16[16,51200]{1,0:T(8,128)(2,1)} reduce(bf16[16,1,51200]{2,1,0:T(2,128)(2,1)S(1)} %all_to_all.16, bf16[]{:T(256)} %broadcast.140), dimensions={1}, to_apply=%all_to_all.16.reduce_sub_computation | reduce | bytes 3276802 | tf_op jit(solution)/shard_map/all_to_all | solution.py:56
  23.7 3.4 reshape.149
  27.1 7.4 %all-to-all-start = ((bf16[16,2,25600]{2,1,0:T(2,128)(2,1)}), bf16[16,2,25600]{2,1,0:T(2,128)(2,1)S(1)}, u32[]{:S(2)}, u32[]{:S(2)}) async-start(bf16[16,2,25600]{2,1,0:T(2,128)(2,1)} %reshape.149), calls=%async_computation | async-start | bytes 3276800 | tf_op jit(solution)/shard_map/all_to_all | solution.py:56
  36.0 36.7 %all-to-all-done = bf16[16,2,25600]{2,1,0:T(2,128)(2,1)S(1)} async-done(((bf16[16,2,25600]{2,1,0:T(2,128)(2,1)}), bf16[16,2,25600]{2,1,0:T(2,128)(2,1)S(1)}, u32[]{:S(2)}, u32[]{:S(2)}) %all-to-all-start) | async-done | bytes 1638432 | tf_op jit(solution)/shard_map/all_to_all | solution.py:56
  72.7 6.2 %reshape.150 = bf16[16,1,51200]{2,1,0:T(2,128)(2,1)} reshape(bf16[16,2,25600]{2,1,0:T(2,128)(2,1)S(1)} %all-to-all-done) | data formatting | bytes 3276800
  89.4 58.1 %all_to_all.19 = bf16[16,2,25600]{2,1,0:T(2,128)(2,1)} all-to-all(bf16[16,2,25600]{2,1,0:T(2,128)(2,1)S(1)} %reshape.151), channel_id=1, replica_groups=mesh['dp'=16,'head'=2] {'dp'}, dimensions={0} | all-to-all | bytes 3276800 | tf_op jit(solution)/shard_map/all_to_all | solution.py:58
  147.4 8.0 %reshape.152 = bf16[16,1,51200]{2,1,0:T(2,128)(2,1)S(1)} reshape(bf16[16,2,25600]{2,1,0:T(2,128)(2,1)} %all_to_all.19) | data formatting | bytes 3276800
  155.4 11.1 %reduce = bf16[16,51200]{1,0:T(8,128)(2,1)} reduce(bf16[16,1,51200]{2,1,0:T(2,128)(2,1)S(1)} %reshape.152, bf16[]{:T(256)} %constant.106), dimensions={1}, to_apply=%all_to_all.15.reduce_sub_computation | reduce | bytes 3276802 | tf_op jit(solution)/shard_map/all_to_all | solution.py:58
  172.3 6.4 %copy.47 = bf16[1280,3,512]{0,2,1:T(8,128)(2,1)} copy(bf16[1280,3,512]{2,0,1:T(8,128)(2,1)} %all-gather.9.cloned.1.call-done) | data formatting | bytes 7864320 | tf_op jit(solution)/shard_map/all_gather | solution.py:96
  178.7 36.6 %all-gather.7.cloned.1.call-done = bf16[1280,1280]{1,0:T(8,128)(2,1)} async-done(((bf16[1280,640]{1,0:T(8,128)(2,1)}), bf16[1280,1280]{1,0:T(8,128)(2,1)}) %all-gather.7.cloned.1.call-update) | async-done | bytes 3276816 | tf_op jit(solution)/shard_map/all_gather | solution.py:20
  217.9 2.9 fusion.32
  220.8 7.8 %fusion.36 = f32[1280,3,512]{0,2,1:T(8,128)S(1)} fusion(bf16[1280,3,512]{0,2,1:T(8,128)(2,1)} %copy.47, bf16[1280,1280]{1,0:T(8,128)(2,1)S(1)} %copy-done.2, f32[1280]{0:T(1024)S(1)} %copy-done.8, f32[1280]{0:T(1024)S(1)} %copy-done.9, f32[1280]{0:T(1024)S(1)} %add_rsqrt_fusion.1, f32[1280]{0:T(1024)S(1)} %broadcast_multiply_fusion.1), kind=kOutput, calls=%fused_computation.57 | convolution fusion | flops 5042995200 | bytes 15093760 | tf_op jit(solution)/shard_map/dot_general | solution.py:98
  231.7 5.0 copy.48
  236.7 3.7 copy.50
  240.4 3.8 copy.49
  244.2 6.8 %fusion.54 = (bf16[8,1280,64]{2,1,0:T(8,128)(2,1)S(1)}, bf16[8,1280,64]{2,1,0:T(8,128)(2,1)}) fusion(f32[1280,8,64]{2,0,1:T(8,128)} %copy.48, f32[8,64]{1,0:T(8,128)S(1)} %add.113, f32[1280,8,64]{2,0,1:T(8,128)} %copy.50, f32[8,64]{1,0:T(8,128)S(1)} %add.116), kind=kLoop, calls=%fused_computation.70 | loop fusion | flops 3276800 | bytes 7868416 | tf_op jit(solution)/shard_map/transpose | solution.py:38
  250.9 47.2 %while.10 = (s32[]{:T(128)}, bf16[8,1280,64]{1,2,0:T(8,128)(2,1)}, bf16[8,1280,64]{2,1,0:T(8,128)(2,1)S(1)}, bf16[8,1280,64]{2,1,0:T(8,128)(2,1)}, bf16[8,1280,64]{2,1,0:T(8,128)(2,1)}, /*index=5*/s32[]{:T(128)}) while((s32[]{:T(128)}, bf16[8,1280,64]{1,2,0:T(8,128)(2,1)}, bf16[8,1280,64]{2,1,0:T(8,128)(2,1)S(1)}, ...), condition=%wide.region_7.8_spmd, body=%wide.region_4.7_spmd.sunk | while | flops 429340160 | bytes 20835396 | solution.py:36
  260.0 2.9 fusion.110
  265.9 2.9 fusion.110
  271.7 2.9 fusion.110
  298.2 5.4 convolution_convert_fusion.1
  303.7 44.9 %reduce-scatter.3.cloned.1.call-done = bf16[1280,640]{1,0:T(8,128)(2,1)} async-done(((bf16[2560,640]{1,0:T(8,128)(2,1)}), bf16[1280,640]{1,0:T(8,128)(2,1)}) %reduce-scatter.3.cloned.1.call-update) | async-done | bytes 1638416 | tf_op jit(solution)/shard_map/reduce_scatter | solution.py:113
  348.6 3.1 add_convert_fusion.2
  353.1 45.2 %all-gather.13.cloned.1.call-done = bf16[1280,1280]{1,0:T(8,128)(2,1)} async-done(((bf16[1280,640]{1,0:T(8,128)(2,1)}), bf16[1280,1280]{1,0:T(8,128)(2,1)}) %all-gather.13.cloned.1.call-update) | async-done | bytes 3276816 | tf_op jit(solution)/shard_map/all_gather | solution.py:20
  400.9 2.9 fusion.28
  403.8 59.5 %all-gather.15.cloned.1.call-done = bf16[1280,2560]{1,0:T(8,128)(2,1)} async-done(((bf16[80,2560]{1,0:T(8,128)(2,1)}), bf16[1280,2560]{1,0:T(8,128)(2,1)}) %all-gather.15.cloned.1.call-update) | async-done | bytes 6553616 | tf_op jit(solution)/shard_map/all_gather | solution.py:126
  463.3 40.8 %fusion.16.clone.4 = bf16[1280,2560]{1,0:T(8,128)(2,1)} fusion(f32[2560]{0:T(1024)S(1)} %copy-done.7, bf16[1280,2560]{1,0:T(8,128)(2,1)} %all-gather.15.cloned.1.call-done, bf16[1280,1280]{1,0:T(8,128)(2,1)S(1)} %copy-done.3, f32[1280]{0:T(1024)S(1)} %copy-done.10, f32[1280]{0:T(1024)S(1)} %copy-done.11, f32[1280]{0:T(1024)S(1)} %add_rsqrt_fusion, ...), kind=kOutput, calls=%fused_computation.21.clone.clone.clone.1 | convolution fusion | flops 8614707200 | bytes 16414720 | tf_op jit(solution)/shard_map/dot_general | solution.py:124
  504.1 23.1 %all-gather.17.cloned.1.call-done = bf16[2560,1280]{1,0:T(8,128)(2,1)} async-done(((bf16[160,1280]{1,0:T(8,128)(2,1)}), bf16[2560,1280]{1,0:T(8,128)(2,1)}) %all-gather.17.cloned.1.call-update) | async-done | bytes 6553616 | tf_op jit(solution)/shard_map/all_gather | solution.py:130
  527.2 14.3 %convolution_convert_fusion = bf16[1280,1280]{0,1:T(8,128)(2,1)} fusion(bf16[2560,1280]{1,0:T(8,128)(2,1)} %all-gather.17.cloned.1.call-done, bf16[1280,2560]{1,0:T(8,128)(2,1)} %fusion.16.clone.4), kind=kOutput, calls=%fused_computation.45 | convolution fusion | flops 8390246400 | bytes 16384000 | tf_op jit(solution)/shard_map/dot_general | solution.py:64
  541.5 5.8 copy.53
  547.4 43.8 %reduce-scatter.5.cloned.1.call-done = bf16[1280,640]{1,0:T(8,128)(2,1)} async-done(((bf16[2560,640]{1,0:T(8,128)(2,1)}), bf16[1280,640]{1,0:T(8,128)(2,1)}) %reduce-scatter.5.cloned.1.call-update) | async-done | bytes 1638416 | tf_op jit(solution)/shard_map/reduce_scatter | solution.py:134
  (92 shorter events, 70.6 us)
Async XLA Ops:
  6.5 163.3 %all-gather.11.cloned.1.call-start = ((), (), s32[]{:S(2)}) async-start(), calls=%async_computation.6 | async-start | bytes 1392640 | tf_op jit(solution)/shard_map/all_gather | solution.py:109
  11.6 24.1 %copy-start.12 = (s32[16]{0:T(128)S(1)}, s32[16]{0:T(128)}, u32[]{:S(2)}) copy-start(s32[16]{0:T(128)} %param.29) | copy-start | bytes 196
  27.1 45.6 %all-to-all-start = ((bf16[16,2,25600]{2,1,0:T(2,128)(2,1)}), bf16[16,2,25600]{2,1,0:T(2,128)(2,1)S(1)}, u32[]{:S(2)}, u32[]{:S(2)}) async-start(bf16[16,2,25600]{2,1,0:T(2,128)(2,1)} %reshape.149), calls=%async_computation | async-start | bytes 3276800 | tf_op jit(solution)/shard_map/all_to_all | solution.py:56
  34.5 137.8 %all-gather.9.cloned.1.call-start = ((), (), s32[]{:S(2)}) async-start(), calls=%async_computation.5 | async-start | bytes 4177920 | tf_op jit(solution)/shard_map/all_gather | solution.py:96
  35.3 180.0 %all-gather.7.cloned.1.call-start = ((), (), s32[]{:S(2)}) async-start(), calls=%async_computation.4 | async-start | bytes 4915200 | tf_op jit(solution)/shard_map/all_gather | solution.py:20
  147.4 22.2 %copy-start.4 = (f32[2,512]{1,0:T(2,128)S(1)}, f32[2,512]{1,0:T(2,128)}, u32[]{:S(2)}) copy-start(f32[2,512]{1,0:T(2,128)} %param.20) | copy-start | bytes 12292
  169.4 179.2 %reduce-scatter.3.cloned.1.call-start = ((), (), s32[]{:S(2)}) async-start(), calls=%async_computation.7 | async-start | bytes 4915200 | tf_op jit(solution)/shard_map/reduce_scatter | solution.py:113
  172.3 48.5 %copy-start.8 = (f32[1280]{0:T(1024)S(1)}, f32[1280]{0:T(1024)}, u32[]{:S(2)}) copy-start(f32[1280]{0:T(1024)} %param.18) | copy-start | bytes 15364
  172.3 48.6 %copy-start.9 = (f32[1280]{0:T(1024)S(1)}, f32[1280]{0:T(1024)}, u32[]{:S(2)}) copy-start(f32[1280]{0:T(1024)} %param.17) | copy-start | bytes 15364
  215.3 5.5 copy-start.2
  298.2 50.5 %copy-start = (bf16[1280,640]{1,0:T(8,128)(2,1)S(1)}, bf16[1280,640]{1,0:T(8,128)(2,1)}, u32[]{:S(2)}) copy-start(bf16[1280,640]{1,0:T(8,128)(2,1)} %reshape.122) | copy-start | bytes 4915204
  298.2 50.5 %copy-start.5 = (f32[640]{0:T(1024)S(1)}, f32[640]{0:T(1024)}, u32[]{:S(2)}) copy-start(f32[640]{0:T(1024)} %param.22) | copy-start | bytes 7684
  303.6 159.7 %copy-start.7 = (f32[2560]{0:T(1024)S(1)}, f32[2560]{0:T(1024)}, u32[]{:S(2)}) copy-start(f32[2560]{0:T(1024)} %param.26) | copy-start | bytes 30724
  303.6 159.7 %copy-start.10 = (f32[1280]{0:T(1024)S(1)}, f32[1280]{0:T(1024)}, u32[]{:S(2)}) copy-start(f32[1280]{0:T(1024)} %param.24) | copy-start | bytes 15364
  303.6 159.7 %copy-start.11 = (f32[1280]{0:T(1024)S(1)}, f32[1280]{0:T(1024)}, u32[]{:S(2)}) copy-start(f32[1280]{0:T(1024)} %param.23) | copy-start | bytes 15364
  303.7 94.6 %all-gather.13.cloned.1.call-start = ((), (), s32[]{:S(2)}) async-start(), calls=%async_computation.8 | async-start | bytes 4915200 | tf_op jit(solution)/shard_map/all_gather | solution.py:20
  351.7 111.6 %all-gather.15.cloned.1.call-start = ((), (), s32[]{:S(2)}) async-start(), calls=%async_computation.9 | async-start | bytes 6963200 | tf_op jit(solution)/shard_map/all_gather | solution.py:126
  352.3 174.9 %all-gather.17.cloned.1.call-start = ((), (), s32[]{:S(2)}) async-start(), calls=%async_computation.10 | async-start | bytes 6963200 | tf_op jit(solution)/shard_map/all_gather | solution.py:130
  353.1 238.1 %reduce-scatter.5.cloned.1.call-start = ((), (), s32[]{:S(2)}) async-start(), calls=%async_computation.11 | async-start | bytes 4915200 | tf_op jit(solution)/shard_map/reduce_scatter | solution.py:134
  398.3 65.0 %copy-start.3 = (bf16[1280,1280]{1,0:T(8,128)(2,1)S(1)}, bf16[1280,1280]{1,0:T(8,128)(2,1)}, u32[]{:S(2)}) copy-start(bf16[1280,1280]{1,0:T(8,128)(2,1)} %all-gather.13.cloned.1.call-done) | copy-start | bytes 9830404
  541.5 49.6 %copy-start.1 = (bf16[1280,640]{1,0:T(8,128)(2,1)S(1)}, bf16[1280,640]{1,0:T(8,128)(2,1)}, u32[]{:S(2)}) copy-start(bf16[1280,640]{1,0:T(8,128)(2,1)} %add_convert_fusion.2) | copy-start | bytes 4915204
  541.5 49.6 %copy-start.6 = (f32[640]{0:T(1024)S(1)}, f32[640]{0:T(1024)}, u32[]{:S(2)}) copy-start(f32[640]{0:T(1024)} %param.28) | copy-start | bytes 7684
Sparse Core Ops, SparseCore 0:
  9.6 48.2 all-gather.10
  60.2 57.7 all-gather.8
  169.5 45.7 all-gather.6
  303.7 44.8 reduce-scatter.2
  351.9 46.3 all-gather.12
  400.4 62.8 all-gather.14
  465.6 61.5 all-gather.16
  547.5 43.6 reduce-scatter.4
where the time goes:
time: 612 us; the launch traced here: 602 us
  waiting for transfers between devices  292 us (48%)
  matrix products  108 us (18%)
  local copies, waits for them, and re-layouts  64.6 us (11%)
  blocking collectives  58.1 us (9%)
  other arithmetic  57.1 us (9%)
  between operations  14.2 us (2%)
  starting transfers between devices  8.18 us (1%)
    all_gather x2, waiting for transfers between devices, normalize(): whole_rows = lax.all_gather(residual_in, 'head', axis=1, tiled=True)  81.8 us
    all_gather x1, waiting for transfers between devices, on_device(): lax.all_gather(fc1_weight, 'dp', axis=0, tiled=True)  59.5 us
    all_to_all x1, blocking collectives, regroup(): lax.all_to_all(picked, 'dp', split_axis=0, concat_axis=0, tiled=True)  58.1 us
    reduce_scatter x1, waiting for transfers between devices, on_device(): lax.psum_scatter(block_term(context, output_rows, frame_count * lax.axis_...  44.9 us
    reduce_scatter x1, waiting for transfers between devices, on_device(): lax.psum_scatter(block_term(hidden, down_rows, frame_count * lax.axis_siz...  43.8 us
    dot_general x1, matrix products, on_device(): jnp.dot(operand, lax.all_gather(fc1_weight, 'dp', axis=0, tiled=True), pr...  40.8 us
    all_to_all x1, waiting for transfers between devices, regroup(): lax.all_to_all(piece_rows, 'dp', split_axis=0, concat_axis=0, tiled=True)  36.7 us
    dot_general x8, matrix products, single(): jnp.dot(probability, value_head, preferred_element_type=jnp.float32)  23.2 us
  transfers between devices with their start and end apart: 9, of which 7 were waited for; matrix products, arithmetic and copies ran while one was open for 18% of the time, Pallas kernels for 0%

commit v1 on v0

--- a/solution.py
+++ b/solution.py
@@ -5,6 +5,13 @@
 
 HDIM = 64
 epsilon = 1e-05
+
+
+def find_arrays(block_in, dim_no=0):
+    arr_out = jnp.stack([block_in for _ in range(jax.lax.axis_size("dp"))], 0)
+    return jnp.concatenate(
+        jax.lax.all_to_all(arr_out, axis_name="dp", split_axis=0, concat_axis=0), dim_no
+    )
 
 
 def layer_norm(matrix, gain_row, shift_row):
@@ -121,11 +128,7 @@
     ).astype(jnp.bfloat16)
     normed_two = normalize(attended, ln2_gain, ln2_bias)
     operand = normed_two
-    hidden_sums = jnp.dot(
-        operand,
-        lax.all_gather(fc1_weight, "dp", axis=0, tiled=True),
-        preferred_element_type=jnp.float32,
-    )
+    hidden_sums = jnp.dot(operand, find_arrays(fc1_weight), preferred_element_type=jnp.float32)
     hidden = jax.nn.gelu(hidden_sums + fc1_bias, approximate=False).astype(jnp.bfloat16)
     down_rows = lax.all_gather(fc2_weight, "dp", axis=0, tiled=True)
     kept = attended.astype(jnp.float32) + fc2_bias

time: 612 us -> 549 us (0.90)
  waiting for transfers between devices: 292 us -> 220 us
    all_gather x1 -> x0, waiting for transfers between devices: 59.5 us -> none  [on_device(): lax.all_gather(fc1_weight, 'dp', axis=0, tiled=True)]
    all_gather x2, waiting for transfers between devices: 81.8 us -> 73.5 us  [normalize(): whole_rows = lax.all_gather(residual_in, 'head', axis=1, tiled=True)]
  transfers between devices with their start and end apart: 9 -> 9, of which waited for: 7 -> 6; matrix products, arithmetic and copies ran while one was open for 18% -> 38% of each run, Pallas kernels for 0% -> 0%
where the time goes in v1:
time: 549 us; the launch traced here: 538 us
  waiting for transfers between devices  220 us (40%)
  matrix products  107 us (19%)
  local copies, waits for them, and re-layouts  68.7 us (13%)
  blocking collectives  58 us (11%)
  other arithmetic  57.1 us (10%)
  between operations  14.2 us (3%)
  starting transfers between devices  13 us (2%)
    all_gather x2, waiting for transfers between devices, normalize(): whole_rows = lax.all_gather(residual_in, 'head', axis=1, tiled=True)  73.5 us
    all_to_all x1, blocking collectives, regroup(): lax.all_to_all(picked, 'dp', split_axis=0, concat_axis=0, tiled=True)  58 us
    reduce_scatter x1, waiting for transfers between devices, on_device(): lax.psum_scatter(block_term(context, output_rows, frame_count * lax.axis_...  44.9 us
    reduce_scatter x1, waiting for transfers between devices, on_device(): lax.psum_scatter(block_term(hidden, down_rows, frame_count * lax.axis_siz...  43.8 us
    dot_general x1, matrix products, on_device(): jnp.dot(operand, find_arrays(fc1_weight), preferred_element_type=jnp.floa...  40.8 us
    all_to_all x1, waiting for transfers between devices, regroup(): lax.all_to_all(piece_rows, 'dp', split_axis=0, concat_axis=0, tiled=True)  36.7 us
    dot_general x8, matrix products, single(): jnp.dot(probability, value_head, preferred_element_type=jnp.float32)  23.2 us
    unnamed x31, local copies, waits for them, and re-layouts  21.9 us
  transfers between devices with their start and end apart: 9, of which 6 were waited for; matrix products, arithmetic and copies ran while one was open for 38% of the time, Pallas kernels for 0%

profile of v1, /device:TPU:0, one launch (start us, length us, event | category | flops | bytes accessed | tf_op | source)
XLA Modules:
  0.0 538.3 jit_solution(9228253219716900360)
XLA Ops:
  7.3 4.3 all_to_all.20
  12.1 11.7 %reduce.9 = bf16[16,51200]{1,0:T(8,128)(2,1)} reduce(bf16[16,1,51200]{2,1,0:T(2,128)(2,1)S(1)} %all_to_all.20, bf16[]{:T(256)} %broadcast.142), dimensions={1}, to_apply=%all_to_all.20.reduce_sub_computation | reduce | bytes 3276802 | tf_op jit(solution)/shard_map/all_to_all | solution.py:63
  23.8 3.4 reshape.155
  27.2 7.4 %all-to-all-start = ((bf16[16,2,25600]{2,1,0:T(2,128)(2,1)}), bf16[16,2,25600]{2,1,0:T(2,128)(2,1)S(1)}, u32[]{:S(2)}, u32[]{:S(2)}) async-start(bf16[16,2,25600]{2,1,0:T(2,128)(2,1)} %reshape.155), calls=%async_computation | async-start | bytes 3276800 | tf_op jit(solution)/shard_map/all_to_all | solution.py:63
  36.0 36.7 %all-to-all-done = bf16[16,2,25600]{2,1,0:T(2,128)(2,1)S(1)} async-done(((bf16[16,2,25600]{2,1,0:T(2,128)(2,1)}), bf16[16,2,25600]{2,1,0:T(2,128)(2,1)S(1)}, u32[]{:S(2)}, u32[]{:S(2)}) %all-to-all-start) | async-done | bytes 1638432 | tf_op jit(solution)/shard_map/all_to_all | solution.py:63
  72.7 6.2 %reshape.156 = bf16[16,1,51200]{2,1,0:T(2,128)(2,1)} reshape(bf16[16,2,25600]{2,1,0:T(2,128)(2,1)S(1)} %all-to-all-done) | data formatting | bytes 3276800
  89.5 58.0 %all_to_all.24 = bf16[16,2,25600]{2,1,0:T(2,128)(2,1)} all-to-all(bf16[16,2,25600]{2,1,0:T(2,128)(2,1)S(1)} %reshape.157), channel_id=1, replica_groups=mesh['dp'=16,'head'=2] {'dp'}, dimensions={0} | all-to-all | bytes 3276800 | tf_op jit(solution)/shard_map/all_to_all | solution.py:65
  147.5 8.0 %reshape.158 = bf16[16,1,51200]{2,1,0:T(2,128)(2,1)S(1)} reshape(bf16[16,2,25600]{2,1,0:T(2,128)(2,1)} %all_to_all.24) | data formatting | bytes 3276800
  155.5 11.1 %reduce = bf16[16,51200]{1,0:T(8,128)(2,1)} reduce(bf16[16,1,51200]{2,1,0:T(2,128)(2,1)S(1)} %reshape.158, bf16[]{:T(256)} %constant.106), dimensions={1}, to_apply=%all_to_all.18.reduce_sub_computation | reduce | bytes 3276802 | tf_op jit(solution)/shard_map/all_to_all | solution.py:65
  169.5 4.3 stack.2
  173.8 4.8 all-to-all-start.2
  181.6 6.2 %copy.47 = bf16[1280,3,512]{0,2,1:T(8,128)(2,1)} copy(bf16[1280,3,512]{2,0,1:T(8,128)(2,1)} %all-gather.8.cloned.1.call-done) | data formatting | bytes 7864320 | tf_op jit(solution)/shard_map/all_gather | solution.py:103
  187.8 27.6 %all-gather.6.cloned.1.call-done = bf16[1280,1280]{1,0:T(8,128)(2,1)} async-done(((bf16[1280,640]{1,0:T(8,128)(2,1)}), bf16[1280,1280]{1,0:T(8,128)(2,1)}) %all-gather.6.cloned.1.call-update) | async-done | bytes 3276816 | tf_op jit(solution)/shard_map/all_gather | solution.py:27
  218.0 2.9 fusion.32
  220.9 7.8 %fusion.36 = f32[1280,3,512]{0,2,1:T(8,128)S(1)} fusion(bf16[1280,3,512]{0,2,1:T(8,128)(2,1)} %copy.47, bf16[1280,1280]{1,0:T(8,128)(2,1)S(1)} %copy-done.2, f32[1280]{0:T(1024)S(1)} %copy-done.8, f32[1280]{0:T(1024)S(1)} %copy-done.9, f32[1280]{0:T(1024)S(1)} %add_rsqrt_fusion.1, f32[1280]{0:T(1024)S(1)} %broadcast_multiply_fusion.1), kind=kOutput, calls=%fused_computation.57 | convolution fusion | flops 5042995200 | bytes 15093760 | tf_op jit(solution)/shard_map/dot_general | solution.py:105
  231.7 5.0 copy.48
  236.7 3.7 copy.50
  240.4 3.8 copy.49
  244.2 6.8 %fusion.54 = (bf16[8,1280,64]{2,1,0:T(8,128)(2,1)S(1)}, bf16[8,1280,64]{2,1,0:T(8,128)(2,1)}) fusion(f32[1280,8,64]{2,0,1:T(8,128)} %copy.48, f32[8,64]{1,0:T(8,128)S(1)} %add.113, f32[1280,8,64]{2,0,1:T(8,128)} %copy.50, f32[8,64]{1,0:T(8,128)S(1)} %add.116), kind=kLoop, calls=%fused_computation.70 | loop fusion | flops 3276800 | bytes 7868416 | tf_op jit(solution)/shard_map/transpose | solution.py:45
  251.0 47.2 %while.10 = (s32[]{:T(128)}, bf16[8,1280,64]{1,2,0:T(8,128)(2,1)}, bf16[8,1280,64]{2,1,0:T(8,128)(2,1)S(1)}, bf16[8,1280,64]{2,1,0:T(8,128)(2,1)}, bf16[8,1280,64]{2,1,0:T(8,128)(2,1)}, /*index=5*/s32[]{:T(128)}) while((s32[]{:T(128)}, bf16[8,1280,64]{1,2,0:T(8,128)(2,1)}, bf16[8,1280,64]{2,1,0:T(8,128)(2,1)S(1)}, ...), condition=%wide.region_7.8_spmd, body=%wide.region_4.7_spmd.sunk | while | flops 429340160 | bytes 20835396 | solution.py:43
  260.0 2.9 fusion.110
  277.7 2.9 fusion.110
  298.2 5.4 %convolution_convert_fusion.1 = bf16[1280,2,640]{2,0,1:T(8,128)(2,1)} fusion(bf16[1280,512,1]{0,1,2:T(8,128)(2,1)} %bitcast.19, bf16[2,640,512]{2,1,0:T(8,128)(2,1)} %bitcast.87), kind=kOutput, calls=%fused_computation.56 | convolution fusion | flops 1679360000 | bytes 5898240 | tf_op jit(solution)/shard_map/dot_general | solution.py:71
  303.8 44.9 %reduce-scatter.3.cloned.1.call-done = bf16[1280,640]{1,0:T(8,128)(2,1)} async-done(((bf16[2560,640]{1,0:T(8,128)(2,1)}), bf16[1280,640]{1,0:T(8,128)(2,1)}) %reduce-scatter.3.cloned.1.call-update) | async-done | bytes 1638416 | tf_op jit(solution)/shard_map/reduce_scatter | solution.py:120
  348.7 3.1 add_convert_fusion.2
  352.4 45.9 %all-gather.12.cloned.1.call-done = bf16[1280,1280]{1,0:T(8,128)(2,1)} async-done(((bf16[1280,640]{1,0:T(8,128)(2,1)}), bf16[1280,1280]{1,0:T(8,128)(2,1)}) %all-gather.12.cloned.1.call-update) | async-done | bytes 3276816 | tf_op jit(solution)/shard_map/all_gather | solution.py:27
  400.9 2.9 fusion.28
  403.9 40.8 %fusion.16.clone.4 = bf16[1280,2560]{1,0:T(8,128)(2,1)} fusion(f32[2560]{0:T(1024)S(1)} %copy-done.7, bf16[1280,2560]{1,0:T(8,128)(2,1)} %bitcast.24, bf16[1280,1280]{1,0:T(8,128)(2,1)S(1)} %copy-done.3, f32[1280]{0:T(1024)S(1)} %copy-done.10, f32[1280]{0:T(1024)S(1)} %copy-done.11, f32[1280]{0:T(1024)S(1)} %add_rsqrt_fusion, ...), kind=kOutput, calls=%fused_computation.21.clone.clone.clone.1 | convolution fusion | flops 8614707200 | bytes 16414720 | tf_op jit(solution)/shard_map/dot_general | solution.py:131
  444.7 18.6 %all-gather.14.cloned.1.call-done = bf16[2560,1280]{1,0:T(8,128)(2,1)} async-done(((bf16[160,1280]{1,0:T(8,128)(2,1)}), bf16[2560,1280]{1,0:T(8,128)(2,1)}) %all-gather.14.cloned.1.call-update) | async-done | bytes 6553616 | tf_op jit(solution)/shard_map/all_gather | solution.py:133
  463.4 14.3 %convolution_convert_fusion = bf16[1280,1280]{0,1:T(8,128)(2,1)} fusion(bf16[2560,1280]{1,0:T(8,128)(2,1)} %all-gather.14.cloned.1.call-done, bf16[1280,2560]{1,0:T(8,128)(2,1)} %fusion.16.clone.4), kind=kOutput, calls=%fused_computation.45 | convolution fusion | flops 8390246400 | bytes 16384000 | tf_op jit(solution)/shard_map/dot_general | solution.py:71
  477.6 5.7 %copy.53 = bf16[2,1280,640]{2,1,0:T(8,128)(2,1)} copy(bf16[2,1280,640]{1,2,0:T(8,128)(2,1)} %bitcast.85) | data formatting | bytes 6553600 | tf_op jit(solution)/shard_map/convert_element_type | solution.py:140
  483.4 43.8 %reduce-scatter.5.cloned.1.call-done = bf16[1280,640]{1,0:T(8,128)(2,1)} async-done(((bf16[2560,640]{1,0:T(8,128)(2,1)}), bf16[1280,640]{1,0:T(8,128)(2,1)}) %reduce-scatter.5.cloned.1.call-update) | async-done | bytes 1638416 | tf_op jit(solution)/shard_map/reduce_scatter | solution.py:137
  (92 shorter events, 72.8 us)
Async XLA Ops:
  6.5 172.5 %all-gather.10.cloned.1.call-start = ((), (), s32[]{:S(2)}) async-start(), calls=%async_computation.7 | async-start | bytes 1392640 | tf_op jit(solution)/shard_map/all_gather | solution.py:116
  11.6 24.1 %copy-start.12 = (s32[16]{0:T(128)S(1)}, s32[16]{0:T(128)}, u32[]{:S(2)}) copy-start(s32[16]{0:T(128)} %param.29) | copy-start | bytes 196
  27.2 45.6 %all-to-all-start = ((bf16[16,2,25600]{2,1,0:T(2,128)(2,1)}), bf16[16,2,25600]{2,1,0:T(2,128)(2,1)S(1)}, u32[]{:S(2)}, u32[]{:S(2)}) async-start(bf16[16,2,25600]{2,1,0:T(2,128)(2,1)} %reshape.155), calls=%async_computation | async-start | bytes 3276800 | tf_op jit(solution)/shard_map/all_to_all | solution.py:63
  34.6 147.0 %all-gather.8.cloned.1.call-start = ((), (), s32[]{:S(2)}) async-start(), calls=%async_computation.6 | async-start | bytes 4177920 | tf_op jit(solution)/shard_map/all_gather | solution.py:103
  35.3 180.1 %all-gather.6.cloned.1.call-start = ((), (), s32[]{:S(2)}) async-start(), calls=%async_computation.5 | async-start | bytes 4915200 | tf_op jit(solution)/shard_map/all_gather | solution.py:27
  173.8 5.1 copy-start.4
  173.8 230.0 %all-to-all-start.2 = ((bf16[16,80,2560]{2,1,0:T(8,128)(2,1)}), bf16[16,80,2560]{2,1,0:T(8,128)(2,1)}, u32[]{:S(2)}, u32[]{:S(2)}) async-start(bf16[16,80,2560]{2,1,0:T(8,128)(2,1)} %stack.2), calls=%async_computation.3 | async-start | bytes 13107200 | tf_op jit(solution)/shard_map/all_to_all | solution.py:13
  178.6 170.0 %reduce-scatter.3.cloned.1.call-start = ((), (), s32[]{:S(2)}) async-start(), calls=%async_computation.8 | async-start | bytes 4915200 | tf_op jit(solution)/shard_map/reduce_scatter | solution.py:120
  181.6 39.4 %copy-start.8 = (f32[1280]{0:T(1024)S(1)}, f32[1280]{0:T(1024)}, u32[]{:S(2)}) copy-start(f32[1280]{0:T(1024)} %param.18) | copy-start | bytes 15364
  181.6 39.4 %copy-start.9 = (f32[1280]{0:T(1024)S(1)}, f32[1280]{0:T(1024)}, u32[]{:S(2)}) copy-start(f32[1280]{0:T(1024)} %param.17) | copy-start | bytes 15364
  215.4 5.5 %copy-start.2 = (bf16[1280,1280]{1,0:T(8,128)(2,1)S(1)}, bf16[1280,1280]{1,0:T(8,128)(2,1)}, u32[]{:S(2)}) copy-start(bf16[1280,1280]{1,0:T(8,128)(2,1)} %all-gather.6.cloned.1.call-done) | copy-start | bytes 9830404
  298.2 50.5 %copy-start = (bf16[1280,640]{1,0:T(8,128)(2,1)S(1)}, bf16[1280,640]{1,0:T(8,128)(2,1)}, u32[]{:S(2)}) copy-start(bf16[1280,640]{1,0:T(8,128)(2,1)} %reshape.127) | copy-start | bytes 4915204
  298.2 50.5 %copy-start.5 = (f32[640]{0:T(1024)S(1)}, f32[640]{0:T(1024)}, u32[]{:S(2)}) copy-start(f32[640]{0:T(1024)} %param.22) | copy-start | bytes 7684
  303.7 100.2 %copy-start.7 = (f32[2560]{0:T(1024)S(1)}, f32[2560]{0:T(1024)}, u32[]{:S(2)}) copy-start(f32[2560]{0:T(1024)} %param.26) | copy-start | bytes 30724
  303.7 100.2 %copy-start.10 = (f32[1280]{0:T(1024)S(1)}, f32[1280]{0:T(1024)}, u32[]{:S(2)}) copy-start(f32[1280]{0:T(1024)} %param.24) | copy-start | bytes 15364
  303.7 100.2 %copy-start.11 = (f32[1280]{0:T(1024)S(1)}, f32[1280]{0:T(1024)}, u32[]{:S(2)}) copy-start(f32[1280]{0:T(1024)} %param.23) | copy-start | bytes 15364
  303.7 94.6 %all-gather.12.cloned.1.call-start = ((), (), s32[]{:S(2)}) async-start(), calls=%async_computation.9 | async-start | bytes 4915200 | tf_op jit(solution)/shard_map/all_gather | solution.py:27
  351.8 111.5 %all-gather.14.cloned.1.call-start = ((), (), s32[]{:S(2)}) async-start(), calls=%async_computation.10 | async-start | bytes 6963200 | tf_op jit(solution)/shard_map/all_gather | solution.py:133
  352.4 174.8 %reduce-scatter.5.cloned.1.call-start = ((), (), s32[]{:S(2)}) async-start(), calls=%async_computation.11 | async-start | bytes 4915200 | tf_op jit(solution)/shard_map/reduce_scatter | solution.py:137
  398.3 5.6 %copy-start.3 = (bf16[1280,1280]{1,0:T(8,128)(2,1)S(1)}, bf16[1280,1280]{1,0:T(8,128)(2,1)}, u32[]{:S(2)}) copy-start(bf16[1280,1280]{1,0:T(8,128)(2,1)} %all-gather.12.cloned.1.call-done) | copy-start | bytes 9830404
  477.6 49.5 %copy-start.1 = (bf16[1280,640]{1,0:T(8,128)(2,1)S(1)}, bf16[1280,640]{1,0:T(8,128)(2,1)}, u32[]{:S(2)}) copy-start(bf16[1280,640]{1,0:T(8,128)(2,1)} %add_convert_fusion.2) | copy-start | bytes 4915204
  477.6 49.5 %copy-start.6 = (f32[640]{0:T(1024)S(1)}, f32[640]{0:T(1024)}, u32[]{:S(2)}) copy-start(f32[640]{0:T(1024)} %param.28) | copy-start | bytes 7684
Sparse Core Ops, SparseCore 0:
  9.6 48.2 all-gather.9
  60.2 57.7 all-gather.7
  169.6 45.7 all-gather.5
  303.8 44.8 reduce-scatter.2
  351.9 46.3 all-gather.11
  400.5 62.8 all-gather.13
  483.5 43.6 reduce-scatter.4
